TPU v7x, 32 devices: a whole 2x2x4 slice. The times are simulated.
32 devices in a mesh: row: 8 (over z, x), col: 4 (over y, core).
Axes of the slice: x: 2, y: 2, z: 4, core: 2. Of those that a mesh axis runs over, the one named last changes fastest.
Arguments:
- trailing: float32 [16384, 8192], P('row', 'col'), may hold values from -6 to 6
- vectors: float32 [16384, 256], P(('row', 'col')), may hold values from -0.1875 to 0.1875
- tfactor: float32 [256, 256], replicated, may hold values from -0.375 to 0.375
Outputs:
- updated: float32 [16384, 8192], P('row', 'col')
All inputs are finite; a program needn't handle non-finite values.
Results may differ from a plain program's by a relative error of at most 0.0003.
Values sent between devices are 32-bit elements.
A program may use at most 128 MiB of HBM per device.

v0:
```python
import jax
import jax.numpy as jnp
from jax import lax
from jax.sharding import PartitionSpec as P


def shards(trailing, vectors, tfactor):
    high = lax.Precision.HIGHEST
    near_vectors = lax.all_gather(vectors, "col", axis=0, tiled=True)
    partial_value = jnp.dot(
        near_vectors.T, trailing, precision=high, preferred_element_type=jnp.float32
    )
    summed = lax.psum(partial_value, "row")
    scaled = jnp.dot(tfactor, summed, precision=high, preferred_element_type=jnp.float32)
    change = jnp.dot(near_vectors, scaled, precision=high, preferred_element_type=jnp.float32)
    return trailing - change


def solution(mesh):
    placed = (P("row", "col"), P(("row", "col"), None), P())
    return jax.shard_map(
        shards, mesh=mesh, in_specs=placed, out_specs=P("row", "col"), check_vma=False
    )
```

profile of v0, /device:TPU:0, one launch (start us, length us, event | category | flops | bytes accessed | tf_op | source)
XLA Modules:
  0.0 203.2 jit_solution(18051398769543396435)
XLA Ops:
  6.5 0.0 copy-start
  6.5 0.0 all-gather.2.cloned.1.call-start
  6.5 0.7 all-gather.2.cloned.1.call-update
  7.3 0.0 all-reduce.2.cloned.1.call-start
  7.3 26.9 %all-gather.2.cloned.1.call-done = f32[2048,256]{1,0:T(8,128)} async-done(((f32[512,256]{1,0:T(8,128)}), f32[2048,256]{1,0:T(8,128)}) %all-gather.2.cloned.1.call-update) | async-done | bytes 2097168 | tf_op jit(solution)/shard_map/all_gather | solution.py:9
  34.2 18.3 %fusion = f32[256,2048]{1,0:T(8,128)} fusion(f32[2048,256]{1,0:T(8,128)} %all-gather.2.cloned.1.call-done, f32[2048,2048]{1,0:T(8,128)} %param.3), kind=kOutput, calls=%fused_computation.1 | convolution fusion | flops 12884901888 | bytes 20971520 | tf_op jit(solution)/shard_map/dot_general | solution.py:10
  52.5 0.0 all-reduce.2.cloned.1.call-update
  52.5 17.7 %copy.4 = f32[2048,2048]{0,1:T(8,128)} copy(f32[2048,2048]{1,0:T(8,128)} %param.3) | data formatting | bytes 33554432 | tf_op args[0]
  70.2 0.0 copy-start.2
  70.2 84.8 %all-reduce.2.cloned.1.call-done = f32[256,2048]{1,0:T(8,128)} async-done(((f32[256,2048]{1,0:T(8,128)}), f32[256,2048]{1,0:T(8,128)}) %all-reduce.2.cloned.1.call-update) | async-done | bytes 2097168 | tf_op jit(solution)/shard_map/psum | solution.py:13
  155.0 0.0 copy-done
  155.0 5.2 %fusion.1 = f32[2048,256]{1,0:T(8,128)S(1)} fusion(f32[256,2048]{1,0:T(8,128)} %all-reduce.2.cloned.1.call-done, f32[256,256]{1,0:T(8,128)S(1)} %copy-done), kind=kOutput, calls=%fused_computation.2 | convolution fusion | flops 1610612736 | bytes 4456448 | tf_op jit(solution)/shard_map/dot_general | solution.py:14
  160.2 0.0 copy-done.2
  160.2 18.5 %bitcast_subtract_fusion = f32[2048,2048]{0,1:T(8,128)} fusion(f32[2048,2048]{0,1:T(8,128)} %copy.4, f32[2048,256]{1,0:T(8,128)S(1)} %fusion.1, f32[2048,256]{1,0:T(8,128)S(1)} %copy-done.2), kind=kOutput, calls=%fused_computation | convolution fusion | flops 12889096192 | bytes 37748736 | tf_op jit(solution)/shard_map/dot_general | solution.py:15
  178.7 0.0 copy-start.1
  178.7 17.6 %copy.5 = f32[2048,2048]{1,0:T(8,128)} copy(f32[2048,2048]{0,1:T(8,128)} %bitcast_subtract_fusion) | data formatting | bytes 33554432 | tf_op jit(solution)/shard_map/sub | solution.py:16
  196.3 0.0 copy-done.1
Async XLA Ops:
  6.5 148.5 %copy-start = (f32[256,256]{1,0:T(8,128)S(1)}, f32[256,256]{1,0:T(8,128)}, u32[]{:S(2)}) copy-start(f32[256,256]{1,0:T(8,128)} %param.5) | copy-start | bytes 786436
  6.5 27.7 %all-gather.2.cloned.1.call-start = ((), (), s32[]{:S(2)}) async-start(), calls=%async_computation | async-start | bytes 2621440 | tf_op jit(solution)/shard_map/all_gather | solution.py:9
  7.3 147.7 %all-reduce.2.cloned.1.call-start = ((), (), s32[]{:S(2)}) async-start(), calls=%async_computation.1 | async-start | bytes 4194304 | tf_op jit(solution)/shard_map/psum | solution.py:13
  70.2 90.0 %copy-start.2 = (f32[2048,256]{1,0:T(8,128)S(1)}, f32[2048,256]{1,0:T(8,128)}, u32[]{:S(2)}) copy-start(f32[2048,256]{1,0:T(8,128)} %all-gather.2.cloned.1.call-done) | copy-start | bytes 6291460
  178.7 17.6 %copy-start.1 = (f32[256,256]{1,0:T(8,128)S(1)}, f32[256,256]{1,0:T(8,128)}, u32[]{:S(2)}) copy-start(f32[256,256]{1,0:T(8,128)} %param.5) | copy-start | bytes 786436
Sparse Core Ops, SparseCore 0:
  8.9 25.2 all-gather.1
  52.7 102.2 all-reduce.1
where the time goes:
time: 204 us; the launch traced here: 203 us
  waiting for transfers between devices  112 us (55%)
  matrix products  42 us (21%)
  local copies, waits for them, and re-layouts  35.3 us (17%)
  between operations  13.4 us (7%)
    psum x1, waiting for transfers between devices, shards(): summed = lax.psum(partial_value, 'row')  84.8 us
    all_gather x1, waiting for transfers between devices, shards(): near_vectors = lax.all_gather(vectors, 'col', axis=0, tiled=True)  26.9 us
    dot_general x1, matrix products, shards(): jnp.dot(near_vectors, scaled, precision=high, preferred_element_type=jnp....  18.5 us
    dot_general x1, matrix products, shards(): jnp.dot(near_vectors.T, trailing, precision=high, preferred_element_type=...  18.3 us
    unnamed x7, local copies, waits for them, and re-layouts  17.7 us
    sub x1, local copies, waits for them, and re-layouts, shards(): return trailing - change  17.6 us
    dot_general x1, matrix products, shards(): jnp.dot(tfactor, summed, precision=high, preferred_element_type=jnp.float32)  5.17 us
  transfers between devices with their start and end apart: 2, of which 2 were waited for; matrix products, arithmetic and copies ran while one was open for 9% of the time, Pallas kernels for 0%

commit v1 on v0

--- a/solution.py
+++ b/solution.py
@@ -10,7 +10,9 @@
     partial_value = jnp.dot(
         near_vectors.T, trailing, precision=high, preferred_element_type=jnp.float32
     )
-    summed = lax.psum(partial_value, "row")
+    summed = partial_value
+    for hop in (1, 2, 4):
+        summed = summed + lax.ppermute(summed, "row", [(dev, dev ^ hop) for dev in range(8)])
     scaled = jnp.dot(tfactor, summed, precision=high, preferred_element_type=jnp.float32)
     change = jnp.dot(near_vectors, scaled, precision=high, preferred_element_type=jnp.float32)
     return trailing - change

time: 204 us -> 288 us (1.41)
  waiting for transfers between devices: 112 us -> 191 us
  starting transfers between devices: 0.04 us -> 5.57 us
    ppermute x0 -> x3, waiting for transfers between devices: none -> 164 us  [shards(): lax.ppermute(summed, 'row', [(dev, dev ^ hop) for dev in range(8)])]
    psum x1 -> x0, waiting for transfers between devices: 84.8 us -> none  [shards(): summed = lax.psum(partial_value, 'row')]
    ppermute x0 -> x3, starting transfers between devices: none -> 5.57 us  [shards(): lax.ppermute(summed, 'row', [(dev, dev ^ hop) for dev in range(8)])]
  transfers between devices with their start and end apart: 2 -> 4, of which waited for: 2 -> 4; matrix products, arithmetic and copies ran while one was open for 9% -> 6% of each run, Pallas kernels for 0% -> 0%
where the time goes in v1:
time: 288 us; the launch traced here: 287 us
  waiting for transfers between devices  191 us (66%)
  matrix products  40.7 us (14%)
  local copies, waits for them, and re-layouts  35.2 us (12%)
  between operations  13.4 us (5%)
  starting transfers between devices  5.57 us (2%)
    ppermute x3, waiting for transfers between devices, shards(): lax.ppermute(summed, 'row', [(dev, dev ^ hop) for dev in range(8)])  164 us
    all_gather x1, waiting for transfers between devices, shards(): near_vectors = lax.all_gather(vectors, 'col', axis=0, tiled=True)  27 us
    dot_general x1, matrix products, shards(): jnp.dot(near_vectors, scaled, precision=high, preferred_element_type=jnp....  18.5 us
    sub x1, local copies, waits for them, and re-layouts, shards(): return trailing - change  17.6 us
    unnamed x7, local copies, waits for them, and re-layouts  17.6 us
    dot_general x1, matrix products, shards(): jnp.dot(near_vectors.T, trailing, precision=high, preferred_element_type=...  17 us
  transfers between devices with their start and end apart: 4, of which 4 were waited for; matrix products, arithmetic and copies ran while one was open for 6% of the time, Pallas kernels for 0%

profile of v1, /device:TPU:0, one launch (start us, length us, event | category | flops | bytes accessed | tf_op | source)
XLA Modules:
  0.0 286.9 jit_solution(4681599309310762461)
XLA Ops:
  6.5 0.0 copy-start
  6.5 0.0 all-gather.2.cloned.1.call-start
  6.5 0.7 all-gather.2.cloned.1.call-update
  7.3 27.0 %all-gather.2.cloned.1.call-done = f32[2048,256]{1,0:T(8,128)} async-done(((f32[512,256]{1,0:T(8,128)}), f32[2048,256]{1,0:T(8,128)}) %all-gather.2.cloned.1.call-update) | async-done | bytes 2097168 | tf_op jit(solution)/shard_map/all_gather | solution.py:9
  34.2 17.0 %fusion.2 = f32[256,2048]{1,0:T(8,128)S(1)} fusion(f32[2048,256]{1,0:T(8,128)} %all-gather.2.cloned.1.call-done, f32[2048,2048]{1,0:T(8,128)} %param.3), kind=kOutput, calls=%fused_computation.3 | convolution fusion | flops 12884901888 | bytes 20971520 | tf_op jit(solution)/shard_map/dot_general | solution.py:10
  51.3 1.5 collective-permute-start
  52.8 46.3 %collective-permute-done = f32[256,2048]{1,0:T(8,128)S(1)} collective-permute-done((f32[256,2048]{1,0:T(8,128)S(1)}, f32[256,2048]{1,0:T(8,128)S(1)}, u32[]{:S(2)}, u32[]{:S(2)}) %collective-permute-start) | collective-permute-done | bytes 2097184 | tf_op jit(solution)/shard_map/ppermute | solution.py:15
  99.1 0.3 add.9
  99.4 1.6 collective-permute-start.1
  100.9 45.4 %collective-permute-done.1 = f32[256,2048]{1,0:T(8,128)S(1)} collective-permute-done((f32[256,2048]{1,0:T(8,128)S(1)}, f32[256,2048]{1,0:T(8,128)S(1)}, u32[]{:S(2)}, u32[]{:S(2)}) %collective-permute-start.1) | collective-permute-done | bytes 2097184 | tf_op jit(solution)/shard_map/ppermute | solution.py:15
  146.4 0.3 add.10
  146.6 2.5 collective-permute-start.2
  149.1 17.6 %copy.4 = f32[2048,2048]{0,1:T(8,128)} copy(f32[2048,2048]{1,0:T(8,128)} %param.3) | data formatting | bytes 33554432 | tf_op args[0]
  166.7 0.0 copy-start.2
  166.7 72.0 %collective-permute-done.2 = f32[256,2048]{1,0:T(8,128)} collective-permute-done((f32[256,2048]{1,0:T(8,128)S(1)}, f32[256,2048]{1,0:T(8,128)}, u32[]{:S(2)}, u32[]{:S(2)}) %collective-permute-start.2) | collective-permute-done | bytes 2097184 | tf_op jit(solution)/shard_map/ppermute | solution.py:15
  238.7 0.0 copy-done
  238.7 5.2 %fusion = f32[2048,256]{1,0:T(8,128)S(1)} fusion(f32[256,256]{1,0:T(8,128)S(1)} %copy-done, f32[256,2048]{1,0:T(8,128)S(1)} %add.10, f32[256,2048]{1,0:T(8,128)} %collective-permute-done.2), kind=kOutput, calls=%fused_computation.1 | convolution fusion | flops 1611137024 | bytes 6553600 | tf_op jit(solution)/shard_map/dot_general | solution.py:16
  243.9 0.0 copy-done.2
  243.9 18.5 %bitcast_subtract_fusion = f32[2048,2048]{0,1:T(8,128)} fusion(f32[2048,2048]{0,1:T(8,128)} %copy.4, f32[2048,256]{1,0:T(8,128)S(1)} %fusion, f32[2048,256]{1,0:T(8,128)S(1)} %copy-done.2), kind=kOutput, calls=%fused_computation | convolution fusion | flops 12889096192 | bytes 37748736 | tf_op jit(solution)/shard_map/dot_general | solution.py:17
  262.4 0.0 copy-start.1
  262.4 17.6 %copy.5 = f32[2048,2048]{1,0:T(8,128)} copy(f32[2048,2048]{0,1:T(8,128)} %bitcast_subtract_fusion) | data formatting | bytes 33554432 | tf_op jit(solution)/shard_map/sub | solution.py:18
  280.0 0.0 copy-done.1
Async XLA Ops:
  6.5 232.2 %copy-start = (f32[256,256]{1,0:T(8,128)S(1)}, f32[256,256]{1,0:T(8,128)}, u32[]{:S(2)}) copy-start(f32[256,256]{1,0:T(8,128)} %param.5) | copy-start | bytes 786436
  6.5 27.7 %all-gather.2.cloned.1.call-start = ((), (), s32[]{:S(2)}) async-start(), calls=%async_computation | async-start | bytes 2621440 | tf_op jit(solution)/shard_map/all_gather | solution.py:9
  51.3 47.8 %collective-permute-start = (f32[256,2048]{1,0:T(8,128)S(1)}, f32[256,2048]{1,0:T(8,128)S(1)}, u32[]{:S(2)}, u32[]{:S(2)}) collective-permute-start(f32[256,2048]{1,0:T(8,128)S(1)} %fusion.2), channel_id=1, source_target_pairs={{0,4},{4,0},{8,12},{12,8},{16,20},{20,16},{24,28},{28,24},{1,5},{5... | collective-permute-start | bytes 6291464 | tf_op jit(solution)/shard_map/ppermute | solution.py:15
  99.4 47.0 %collective-permute-start.1 = (f32[256,2048]{1,0:T(8,128)S(1)}, f32[256,2048]{1,0:T(8,128)S(1)}, u32[]{:S(2)}, u32[]{:S(2)}) collective-permute-start(f32[256,2048]{1,0:T(8,128)S(1)} %add.9), channel_id=1, source_target_pairs={{0,8},{4,12},{8,0},{12,4},{16,24},{20,28},{24,16},{28,20},{1,9},{5... | collective-permute-start | bytes 6291464 | tf_op jit(solution)/shard_map/ppermute | solution.py:15
  146.6 92.1 %collective-permute-start.2 = (f32[256,2048]{1,0:T(8,128)S(1)}, f32[256,2048]{1,0:T(8,128)}, u32[]{:S(2)}, u32[]{:S(2)}) collective-permute-start(f32[256,2048]{1,0:T(8,128)S(1)} %add.10), channel_id=1, source_target_pairs={{0,16},{4,20},{8,24},{12,28},{16,0},{20,4},{24,8},{28,12},{1,17},{... | collective-permute-start | bytes 6291464 | tf_op jit(solution)/shard_map/ppermute | solution.py:15
  166.7 77.2 %copy-start.2 = (f32[2048,256]{1,0:T(8,128)S(1)}, f32[2048,256]{1,0:T(8,128)}, u32[]{:S(2)}) copy-start(f32[2048,256]{1,0:T(8,128)} %all-gather.2.cloned.1.call-done) | copy-start | bytes 6291460
  262.4 17.6 %copy-start.1 = (f32[256,256]{1,0:T(8,128)S(1)}, f32[256,256]{1,0:T(8,128)}, u32[]{:S(2)}) copy-start(f32[256,256]{1,0:T(8,128)} %param.5) | copy-start | bytes 786436
Sparse Core Ops, SparseCore 0:
  8.9 25.2 all-gather.1
